TPU v7x, 32 devices: a whole 2x2x4 slice. The times are simulated.
32 devices in a mesh: dp: 8 (over z, core), seq: 4 (over y, x).
Axes of the slice: x: 2, y: 2, z: 4, core: 2. Of those that a mesh axis runs over, the one named last changes fastest.
Arguments:
- tokens: bfloat16 [32, 256, 1024], P(('dp', 'seq')), may hold values from -6 to 6
- queries: bfloat16 [32, 256, 1024], P(('dp', 'seq')), may hold values from -240 to 240
- keys: bfloat16 [32, 256, 1024], P(('dp', 'seq')), may hold values from -7 to 7
- values: bfloat16 [32, 256, 1024], P(('dp', 'seq')), may hold values from -6 to 6
- ln_gain: bfloat16 [1024], replicated, may hold values from 0.5 to 1.5
- mean_in: bfloat16 [1024, 2048], P(None, 'seq'), may hold values from -0.1875 to 0.1875
- sigma_in: bfloat16 [1024, 2048], P(None, 'seq'), may hold values from 0.0039978027 to 0.029907227
- noise_in: bfloat16 [1024, 2048], P(None, 'seq'), may hold values from -4 to 4
- mean_out: bfloat16 [2048, 1024], P('seq'), may hold values from -0.125 to 0.125
- sigma_out: bfloat16 [2048, 1024], P('seq'), may hold values from 0.0019989014 to 0.014953613
- noise_out: bfloat16 [2048, 1024], P('seq'), may hold values from -4 to 4
- flip_in: int32 [32, 1024], P('dp'), may hold values from -1 to 1, as said below
- flip_mid: int32 [32, 2048], P('dp', 'seq'), may hold values from -1 to 1, as said below
- flip_hidden: int32 [32, 2048], P('dp', 'seq'), may hold values from -1 to 1, as said below
- flip_out: int32 [32, 1024], P('dp'), may hold values from -1 to 1, as said below
- cotangent: bfloat16 [32, 256, 1024], P(('dp', 'seq')), may hold values from -0.75 to 0.75
Outputs:
- block_out: bfloat16 [32, 256, 1024], P(('dp', 'seq'))
- resid_grad: bfloat16 [32, 256, 1024], P(('dp', 'seq'))
- grad_mean_in: float32 [1024, 2048], P(None, 'seq')
- grad_sigma_in: float32 [1024, 2048], P(None, 'seq')
- grad_mean_out: float32 [2048, 1024], P('seq')
- grad_sigma_out: float32 [2048, 1024], P('seq')
Inputs may be any that keep to these rules, and one draw needn't show every extreme that they name: `flip_in`: each entry is -1 or +1. `flip_mid`: each entry is -1 or +1. `flip_hidden`: each entry is -1 or +1. `flip_out`: each entry is -1 or +1.
All inputs are finite; a program needn't handle non-finite values.
Results may differ from a plain program's by a relative error of at most 0.018.
Values may be sent and summed in bfloat16 or wider, within the bound.
A program may use at most 128 MiB of HBM per device.

v0:
```python
import jax
import jax.numpy as jnp
from jax import lax
from jax.sharding import PartitionSpec as P

HEADS = 16


def gelu_slope(pre):
    cdf = 0.5 * (1.0 + lax.erf(pre * 0.7071067811865476))
    pdf = jnp.exp(-0.5 * pre * pre) * 0.3989422804014327
    return cdf + pre * pdf


def contract_first(left, right):
    return lax.dot_general(
        left, right, (((0,), (0,)), ((), ())), preferred_element_type=jnp.float32
    )


def contract_last(left, right):
    return lax.dot_general(
        left, right, (((1,), (1,)), ((), ())), preferred_element_type=jnp.float32
    )


def body(
    tokens,
    queries,
    keys,
    values,
    ln_gain,
    mean_in,
    sigma_in,
    noise_in,
    mean_out,
    sigma_out,
    noise_out,
    flip_in,
    flip_mid,
    flip_hidden,
    flip_out,
    cotangent,
):
    bf = jnp.bfloat16
    f32 = jnp.float32
    own_images, patches, width = tokens.shape
    hidden_local = mean_in.shape[1]
    head_dim = width // HEADS
    scale = head_dim ** (-0.5)
    pert_in = (sigma_in.astype(f32) * noise_in.astype(f32)).astype(bf)
    pert_out = (sigma_out.astype(f32) * noise_out.astype(f32)).astype(bf)
    query_heads = queries.reshape(own_images, patches, HEADS, head_dim)
    key_heads = keys.reshape(own_images, patches, HEADS, head_dim)
    value_heads = values.reshape(own_images, patches, HEADS, head_dim)
    scores = (
        jnp.einsum("bqhe,bkhe->bhqk", query_heads, key_heads, preferred_element_type=f32) * scale
    )
    top = jnp.max(scores, axis=-1, keepdims=True)
    expd = jnp.exp(scores - top)
    total = jnp.sum(expd, axis=-1)
    accum = jnp.einsum("bhqk,bkhe->bqhe", expd.astype(bf), value_heads, preferred_element_type=f32)
    attn_out = (
        (accum / jnp.transpose(total, (0, 2, 1))[..., None])
        .reshape(own_images, patches, width)
        .astype(bf)
    )
    resid = (tokens.astype(f32) + attn_out.astype(f32)).astype(bf)
    resid_f = resid.astype(f32)
    centered = resid_f - jnp.mean(resid_f, axis=-1, keepdims=True)
    rstd = lax.rsqrt(jnp.mean(centered * centered, axis=-1, keepdims=True) + 1e-06)
    ahat = centered * rstd
    gain_f = ln_gain.astype(f32)
    normed = (ahat * gain_f).astype(bf)
    in_signs = flip_in.astype(bf)[:, None, :]
    in_signs_f = flip_in.astype(f32)[:, None, :]
    mid_signs = flip_mid.astype(bf)[:, None, :]
    mid_signs_f = flip_mid.astype(f32)[:, None, :]
    hid_signs = flip_hidden.astype(bf)[:, None, :]
    hid_signs_f = flip_hidden.astype(f32)[:, None, :]
    out_signs = flip_out.astype(bf)[:, None, :]
    out_signs_f = flip_out.astype(f32)[:, None, :]
    gathered = lax.all_gather(normed, "seq", axis=0, tiled=True)
    count = gathered.shape[0]
    signs = in_signs
    flat = gathered.reshape(-1, width)
    flat_flip = (gathered * signs).reshape(-1, width)
    plain = jnp.dot(flat, mean_in, preferred_element_type=f32).reshape(count, patches, hidden_local)
    noisy = jnp.dot(flat_flip, pert_in, preferred_element_type=f32).reshape(
        count, patches, hidden_local
    )
    pre = plain + noisy * mid_signs_f
    group_images = pre.shape[0]
    rows = group_images * patches
    hidden = jax.nn.gelu(pre, approximate=False).astype(bf)
    flipped_hidden = hidden * hid_signs
    count = lax.axis_size("seq") * own_images
    hb = hidden.reshape(-1, hidden_local)
    hfb = flipped_hidden.reshape(-1, hidden_local)
    plain = jnp.dot(hb, mean_out, preferred_element_type=f32).reshape(count, patches, width)
    noisy = jnp.dot(hfb, pert_out, preferred_element_type=f32).reshape(count, patches, width)
    mixed = lax.psum_scatter(
        (plain + noisy * out_signs_f).astype(jnp.bfloat16), "seq", scatter_dimension=0, tiled=True
    ).astype(jnp.float32)
    block_out = (resid_f + mixed).astype(bf)
    cot_all = lax.all_gather(cotangent, "seq", axis=0, tiled=True)
    cot_flat = cot_all.reshape(rows, width)
    cot_flip_flat = (cot_all * out_signs).reshape(rows, width)
    dhidden = contract_last(cot_flat, mean_out).reshape(group_images, patches, hidden_local)
    dhidden = (
        dhidden
        + contract_last(cot_flip_flat, pert_out).reshape(group_images, patches, hidden_local)
        * hid_signs_f
    )
    dpre = (dhidden * gelu_slope(pre)).astype(bf)
    dpre_flip = dpre * mid_signs
    local_mean_out = contract_first(hidden.reshape(rows, hidden_local), cot_flat)
    local_sigma_out = contract_first(
        flipped_hidden.reshape(rows, hidden_local), cot_flip_flat
    ) * noise_out.astype(f32)
    grad_mean_out, grad_sigma_out = (
        lax.psum(local_mean_out.astype(jnp.bfloat16), "dp").astype(jnp.float32),
        lax.psum(local_sigma_out.astype(jnp.bfloat16), "dp").astype(jnp.float32),
    )
    local_mean_in = contract_first(gathered.reshape(rows, width), dpre.reshape(rows, hidden_local))
    local_flip_in = contract_first(
        (gathered * in_signs).reshape(rows, width), dpre_flip.reshape(rows, hidden_local)
    )
    local_sigma_in = local_flip_in * noise_in.astype(f32)
    count = lax.axis_size("seq") * own_images
    drows = dpre.reshape(-1, hidden_local)
    dflip_rows = dpre_flip.reshape(-1, hidden_local)
    signs = in_signs_f
    plain = contract_last(drows, mean_in).reshape(count, patches, width)
    noisy = contract_last(dflip_rows, pert_in).reshape(count, patches, width)
    dnormed = lax.psum_scatter(
        (plain + noisy * signs).astype(jnp.bfloat16), "seq", scatter_dimension=0, tiled=True
    ).astype(jnp.float32)
    grad_mean_in, grad_sigma_in = (
        lax.psum(local_mean_in.astype(jnp.bfloat16), "dp").astype(jnp.float32),
        lax.psum(local_sigma_in.astype(jnp.bfloat16), "dp").astype(jnp.float32),
    )
    scaled = dnormed * gain_f
    back = rstd * (
        scaled
        - jnp.mean(scaled, axis=-1, keepdims=True)
        - ahat * jnp.mean(scaled * ahat, axis=-1, keepdims=True)
    )
    resid_grad = (cotangent.astype(f32) + back).astype(bf)
    return (block_out, resid_grad, grad_mean_in, grad_sigma_in, grad_mean_out, grad_sigma_out)


def solution(mesh):
    return jax.shard_map(
        body,
        mesh=mesh,
        in_specs=(
            P(("dp", "seq"), None, None),
            P(("dp", "seq"), None, None),
            P(("dp", "seq"), None, None),
            P(("dp", "seq"), None, None),
            P(),
            P(None, "seq"),
            P(None, "seq"),
            P(None, "seq"),
            P("seq", None),
            P("seq", None),
            P("seq", None),
            P("dp", None),
            P("dp", "seq"),
            P("dp", "seq"),
            P("dp", None),
            P(("dp", "seq"), None, None),
        ),
        out_specs=(
            P(("dp", "seq"), None, None),
            P(("dp", "seq"), None, None),
            P(None, "seq"),
            P(None, "seq"),
            P("seq", None),
            P("seq", None),
        ),
        check_vma=False,
    )
```

profile of v0, /device:TPU:0, one launch (start us, length us, event | category | flops | bytes accessed | tf_op | source)
XLA Modules:
  0.0 289.0 jit_solution(1723222755347720097)
XLA Ops:
  7.2 0.0 copy-start
  7.2 0.0 all-gather.3.cloned.1.call-start
  7.2 1.4 copy.42
  8.6 1.2 copy.40
  9.9 0.0 copy-done.18
  9.9 0.2 copy.41
  10.1 0.8 multiply_reduce_fusion
  10.8 0.7 fusion
  11.6 0.9 divide_convert_fusion
  12.4 0.0 copy-start.19
  12.5 0.1 bitcast_convert_fusion.2
  12.6 1.3 copy.44
  13.9 0.0 copy-done.24
  13.9 0.0 copy-start.23
  13.9 0.0 copy-start.20
  13.9 0.0 copy-start.21
  13.9 0.0 copy-start.7
  13.9 1.5 convert_reduce_fusion
  15.5 0.3 fusion.51
  15.8 1.1 fusion.45
  16.9 0.0 all-gather.3.cloned.1.call-update
  16.9 0.0 all-gather.5.cloned.1.call-start
  16.9 0.7 all-gather.5.cloned.1.call-update
  17.6 0.2 all-reduce.5.cloned.1.call-start
  17.9 0.0 copy-done.20
  18.0 37.0 %all-gather.3.cloned.1.call-done = bf16[4,256,1024]{2,1,0:T(8,128)(2,1)} async-done(((bf16[1,256,1024]{2,1,0:T(8,128)(2,1)}), bf16[4,256,1024]{2,1,0:T(8,128)(2,1)}) %all-gather.3.cloned.1.call-update) | async-done | bytes 2097168 | tf_op jit(solution)/shard_map/all_gather | solution.py:83
  55.0 3.3 %fusion.31 = f32[4,256,512]{2,1,0:T(8,128)S(1)} fusion(bf16[4,256,1024]{2,1,0:T(8,128)(2,1)} %all-gather.3.cloned.1.call-done, bf16[4,1024]{1,0:T(4,128)(2,1)S(1)} %get-tuple-element.19, bf16[1024,512]{1,0:T(8,128)(2,1)S(1)} %copy-done.7, bf16[1024,512]{1,0:T(8,128)(2,1)} %param.22), kind=kOutput, calls=%fused_computation.55 | convolution fusion | flops 1076887552 | bytes 6299648 | tf_op jit(solution)/shard_map/dot_general | solution.py:89
  58.3 1.9 fusion.77
  60.2 0.0 copy-start.4
  60.2 1.3 copy-done.4
  61.5 4.7 %fusion.8 = bf16[4,256,512]{2,1,0:T(8,128)(2,1)S(1)} fusion(f32[4,256,512]{2,1,0:T(8,128)S(1)} %get-tuple-element.28, u8[256,512]{1,0:T(8,128)(4,1)S(1)} %get-tuple-element.7, u8[256,512]{1,0:T(8,128)(4,1)S(1)} %get-tuple-element.6), kind=kLoop, calls=%fused_computation.18 | loop fusion | flops 36700160 | bytes 3407872 | tf_op jit(solution)/shard_map/convert_element_type | solution.py:95
  66.2 25.8 %all-gather.5.cloned.1.call-done = bf16[4,256,1024]{2,1,0:T(8,128)(2,1)} async-done(((bf16[1,256,1024]{2,1,0:T(8,128)(2,1)}), bf16[4,256,1024]{2,1,0:T(8,128)(2,1)}) %all-gather.5.cloned.1.call-update) | async-done | bytes 2097168 | tf_op jit(solution)/shard_map/all_gather | solution.py:106
  92.0 3.6 %fusion.27 = f32[4,256,512]{2,1,0:T(8,128)S(1)} fusion(bf16[4,256,1024]{2,1,0:T(8,128)(2,1)} %all-gather.5.cloned.1.call-done, bf16[4,1024]{1,0:T(4,128)(2,1)S(1)} %get-tuple-element.20, bf16[512,1024]{1,0:T(8,128)(2,1)} %param.26, bf16[512,1024]{1,0:T(8,128)(2,1)} %param.25), kind=kOutput, calls=%fused_computation.51 | convolution fusion | flops 1076887552 | bytes 6299648 | tf_op jit(solution)/shard_map/dot_general | solution.py:22
  95.7 0.1 copy-done.17
  95.8 2.0 fusion.14
  97.8 0.0 copy-start.1
  97.8 0.0 copy-start.8
  97.8 2.3 bitcast_convert_fusion.1
  100.1 2.3 fusion.3
  102.4 2.3 bitcast_convert_fusion
  104.6 2.4 fusion.5
  107.0 0.0 all-reduce.5.cloned.1.call-update
  107.0 0.3 reduce-scatter.9.cloned.1.call-start
  107.3 0.0 copy-start.2
  107.3 0.0 copy-start.9
  107.3 0.0 copy-start.10
  107.3 2.7 fusion.58
  110.0 2.6 add_convert_fusion
  112.6 0.0 reduce-scatter.9.cloned.1.call-update
  112.7 0.0 reduce-scatter.7.cloned.1.call-start
  112.7 0.0 copy-start.12
  112.7 0.0 copy-start.13
  112.7 2.6 fusion.56
  115.4 2.6 add_convert_fusion.1
  118.0 0.0 reduce-scatter.7.cloned.1.call-update
  118.0 85.7 %all-reduce.5.cloned.1.call-done = (bf16[1024,512]{1,0:T(8,128)(2,1)}, bf16[1024,512]{1,0:T(8,128)(2,1)}, bf16[512,1024]{1,0:T(8,128)(2,1)}, bf16[512,1024]{1,0:T(8,128)(2,1)}) async-done(((bf16[1024,512]{1,0:T(8,128)(2,1)}, bf16[1024,512]{1,0:T(8,128)(2,1)}, bf16[512,1024]{1,0:T(8,128)(2,1)}, bf16[512,1024]{1,0:T(8,128)(2,1)}), (bf16[1024,512]{1,0:T(8,128)(2,1)}, bf16[1024,512]{1,0:T(8,128)(2,1)}, ...) | async-done | bytes 4194320 | tf_op jit(solution)/shard_map/psum | solution.py:140
  203.7 2.9 %convert_element_type.173 = f32[1024,512]{1,0:T(8,128)} convert(bf16[1024,512]{1,0:T(8,128)(2,1)} %get-tuple-element.10) | non-fusion elementwise | flops 524288 | bytes 3145728 | tf_op jit(solution)/shard_map/convert_element_type | solution.py:140
  206.7 1.6 convert_element_type.175
  208.3 1.6 convert_element_type.177
  209.8 1.6 convert_element_type.179
  211.4 30.4 %reduce-scatter.9.cloned.1.call-done = bf16[1,256,1024]{2,1,0:T(8,128)(2,1)} async-done(((bf16[4,256,1024]{2,1,0:T(8,128)(2,1)}), bf16[1,256,1024]{2,1,0:T(8,128)(2,1)}) %reduce-scatter.9.cloned.1.call-update) | async-done | bytes 524304
  241.8 1.4 fusion.61
  243.2 36.6 %reduce-scatter.7.cloned.1.call-done = bf16[1,256,1024]{2,1,0:T(8,128)(2,1)} async-done(((bf16[4,256,1024]{2,1,0:T(8,128)(2,1)}), bf16[1,256,1024]{2,1,0:T(8,128)(2,1)}) %reduce-scatter.7.cloned.1.call-update) | async-done | bytes 524304
  279.8 2.6 fusion.50
  (43 shorter events, 0.1 us)
Async XLA Ops:
  7.2 51.1 %copy-start = (bf16[1024,512]{1,0:T(8,128)(2,1)S(1)}, bf16[1024,512]{1,0:T(8,128)(2,1)}, u32[]{:S(2)}) copy-start(bf16[1024,512]{1,0:T(8,128)(2,1)} %param.21) | copy-start | bytes 3145732
  7.2 2.7 copy-start.18
  7.2 47.8 %all-gather.3.cloned.1.call-start = ((), (), s32[]{:S(2)}) async-start(), calls=%async_computation.2 | async-start | bytes 2621440 | tf_op jit(solution)/shard_map/all_gather | solution.py:83
  12.4 1.4 copy-start.24
  12.4 1.4 copy-start.19
  13.9 4.0 %copy-start.22 = (s32[4,512]{1,0:T(4,128)S(1)}, s32[4,512]{1,0:T(4,128)}, u32[]{:S(2)}) copy-start(s32[4,512]{1,0:T(4,128)} %param.28) | copy-start | bytes 24580
  13.9 4.0 %copy-start.23 = (s32[4,512]{1,0:T(4,128)S(1)}, s32[4,512]{1,0:T(4,128)}, u32[]{:S(2)}) copy-start(s32[4,512]{1,0:T(4,128)} %param.29) | copy-start | bytes 24580
  13.9 4.0 %copy-start.20 = (s32[4,1024]{1,0:T(4,128)S(1)}, s32[4,1024]{1,0:T(4,128)}, u32[]{:S(2)}) copy-start(s32[4,1024]{1,0:T(4,128)} %param.27) | copy-start | bytes 49156
  13.9 4.0 %copy-start.21 = (s32[4,1024]{1,0:T(4,128)S(1)}, s32[4,1024]{1,0:T(4,128)}, u32[]{:S(2)}) copy-start(s32[4,1024]{1,0:T(4,128)} %param.30) | copy-start | bytes 49156
  13.9 41.0 %copy-start.7 = (bf16[1024,512]{1,0:T(8,128)(2,1)S(1)}, bf16[1024,512]{1,0:T(8,128)(2,1)}, u32[]{:S(2)}) copy-start(bf16[1024,512]{1,0:T(8,128)(2,1)} %param.23) | copy-start | bytes 3145732
  16.9 75.1 %all-gather.5.cloned.1.call-start = ((), (), s32[]{:S(2)}) async-start(), calls=%async_computation.3 | async-start | bytes 2621440 | tf_op jit(solution)/shard_map/all_gather | solution.py:106
  17.6 186.1 %all-reduce.5.cloned.1.call-start = ((), (), s32[]{:S(2)}) async-start(), calls=%async_computation.6 | async-start | bytes 8388608 | tf_op jit(solution)/shard_map/psum | solution.py:140
  55.0 3.3 %copy-start.25 = (bf16[4,256,1024]{2,1,0:T(8,128)(2,1)S(1)}, bf16[4,256,1024]{2,1,0:T(8,128)(2,1)}, u32[]{:S(2)}) copy-start(bf16[4,256,1024]{2,1,0:T(8,128)(2,1)} %all-gather.3.cloned.1.call-done) | copy-start | bytes 6291460
  60.2 1.3 copy-start.4
  92.0 3.6 %copy-start.3 = (bf16[4,256,1024]{2,1,0:T(8,128)(2,1)S(1)}, bf16[4,256,1024]{2,1,0:T(8,128)(2,1)}, u32[]{:S(2)}) copy-start(bf16[4,256,1024]{2,1,0:T(8,128)(2,1)} %all-gather.5.cloned.1.call-done) | copy-start | bytes 6291460
  92.0 3.6 %copy-start.5 = (f32[4,256,512]{2,1,0:T(8,128)S(1)}, f32[4,256,512]{2,1,0:T(8,128)}, u32[]{:S(2)}) copy-start(f32[4,256,512]{2,1,0:T(8,128)} %copy-done.4) | copy-start | bytes 6291460
  92.0 3.7 %copy-start.17 = (bf16[512,1024]{1,0:T(8,128)(2,1)S(1)}, bf16[512,1024]{1,0:T(8,128)(2,1)}, u32[]{:S(2)}) copy-start(bf16[512,1024]{1,0:T(8,128)(2,1)} %param.24) | copy-start | bytes 3145732
  95.8 2.1 copy-start.26
  97.8 2.3 copy-start.1
  97.8 2.3 copy-start.8
  102.4 2.3 copy-start.11
  107.0 134.8 %reduce-scatter.9.cloned.1.call-start = ((), (), s32[]{:S(2)}) async-start(), calls=%async_computation.5 | async-start | bytes 2621440
  107.3 2.7 copy-start.2
  107.3 2.7 copy-start.9
  107.3 2.7 copy-start.10
  112.7 167.2 %reduce-scatter.7.cloned.1.call-start = ((), (), s32[]{:S(2)}) async-start(), calls=%async_computation.4 | async-start | bytes 2621440
  112.7 2.7 copy-start.12
  112.7 2.7 copy-start.13
  203.7 2.9 %copy-start.16 = (bf16[1024,512]{1,0:T(8,128)(2,1)S(1)}, bf16[1024,512]{1,0:T(8,128)(2,1)}, u32[]{:S(2)}) copy-start(bf16[1024,512]{1,0:T(8,128)(2,1)} %get-tuple-element.11) | copy-start | bytes 3145732
  206.6 1.6 copy-start.15
  208.3 1.6 copy-start.14
  209.8 70.0 %copy-start.6 = (bf16[1,256,1024]{2,1,0:T(8,128)(2,1)S(1)}, bf16[1,256,1024]{2,1,0:T(8,128)(2,1)}, u32[]{:S(2)}) copy-start(bf16[1,256,1024]{2,1,0:T(8,128)(2,1)} %param.31) | copy-start | bytes 1572868
Sparse Core Ops, SparseCore 0:
  17.0 37.8 all-gather.2
  56.8 35.1 all-gather.4
  107.1 96.5 all-reduce.4
  206.5 35.2 reduce-scatter.8
  244.6 35.1 reduce-scatter.6
where the time goes:
time: 289 us
  waiting for transfers between devices  216 us (75%)
  matrix products  32.2 us (11%)
  other arithmetic  20.2 us (7%)
  between operations  14.2 us (5%)
  local copies, waits for them, and re-layouts  5.66 us (2%)
    psum x1, waiting for transfers between devices, body(): lax.psum(local_mean_in.astype(jnp.bfloat16), 'dp').astype(jnp.float32)  85.7 us
    unnamed x7, waiting for transfers between devices  67.8 us
    all_gather x1, waiting for transfers between devices, body(): gathered = lax.all_gather(normed, 'seq', axis=0, tiled=True)  37 us
    all_gather x1, waiting for transfers between devices, body(): cot_all = lax.all_gather(cotangent, 'seq', axis=0, tiled=True)  25.8 us
    dot_general x4, matrix products, contract_last(): lax.dot_general(left, right, (((1,), (1,)), ((), ())), preferred_element_...  11 us
    dot_general x4, matrix products, contract_first(): lax.dot_general(left, right, (((0,), (0,)), ((), ())), preferred_element_...  9.14 us
  transfers between devices with their start and end apart: 5, of which 5 were waited for; matrix products, arithmetic and copies ran while one was open for 10% of the time, Pallas kernels for 0%

commit v1 on v0

--- a/solution.py
+++ b/solution.py
@@ -4,6 +4,16 @@
 from jax.sharding import PartitionSpec as P
 
 HEADS = 16
+
+
+def gather_by_hops(array, axis, along):
+    peers = lax.axis_size(axis)
+    held, pieces = (array, [array])
+    for _ in range(peers - 1):
+        held = lax.ppermute(held, axis, [(i, (i + 1) % peers) for i in range(peers)])
+        pieces.insert(0, held)
+    row_of_blocks = jnp.concatenate(pieces, axis=along)
+    return jnp.roll(row_of_blocks, (lax.axis_index(axis) + 1) * array.shape[along], axis=along)
 
 
 def gelu_slope(pre):
@@ -103,7 +113,7 @@
         (plain + noisy * out_signs_f).astype(jnp.bfloat16), "seq", scatter_dimension=0, tiled=True
     ).astype(jnp.float32)
     block_out = (resid_f + mixed).astype(bf)
-    cot_all = lax.all_gather(cotangent, "seq", axis=0, tiled=True)
+    cot_all = gather_by_hops(cotangent, "seq", 0)
     cot_flat = cot_all.reshape(rows, width)
     cot_flip_flat = (cot_all * out_signs).reshape(rows, width)
     dhidden = contract_last(cot_flat, mean_out).reshape(group_images, patches, hidden_local)

time: 289 us -> 283 us (0.979)
  waiting for transfers between devices: 216 us -> 201 us
  starting transfers between devices: 0.6 us -> 8.38 us
    ppermute x0 -> x3, waiting for transfers between devices: none -> 47.3 us  [gather_by_hops(): lax.ppermute(held, axis, [(i, (i + 1) % peers) for i in range(peers)])]
    all_gather x1, waiting for transfers between devices: 37 us -> 0.01 us  [body(): gathered = lax.all_gather(normed, 'seq', axis=0, tiled=True)]
    all_gather x1 -> x0, waiting for transfers between devices: 25.8 us -> none  [body(): cot_all = lax.all_gather(cotangent, 'seq', axis=0, tiled=True)]
    ppermute x0 -> x3, starting transfers between devices: none -> 7.99 us  [gather_by_hops(): lax.ppermute(held, axis, [(i, (i + 1) % peers) for i in range(peers)])]
    unnamed x57 -> x64, local copies, waits for them, and re-layouts: 4.35 us -> 7.59 us
    unnamed x7 -> x6, waiting for transfers between devices: 67.8 us -> 67.3 us
  transfers between devices with their start and end apart: 5 -> 7, of which waited for: 5 -> 6; matrix products, arithmetic and copies ran while one was open for 10% -> 9% of each run, Pallas kernels for 0% -> 0%
where the time goes in v1:
time: 283 us; the launch traced here: 282 us
  waiting for transfers between devices  201 us (71%)
  matrix products  31.3 us (11%)
  other arithmetic  20 us (7%)
  between operations  14.2 us (5%)
  starting transfers between devices  8.38 us (3%)
  local copies, waits for them, and re-layouts  7.96 us (3%)
    psum x1, waiting for transfers between devices, body(): lax.psum(local_mean_in.astype(jnp.bfloat16), 'dp').astype(jnp.float32)  86.2 us
    unnamed x6, waiting for transfers between devices  67.3 us
    ppermute x3, waiting for transfers between devices, gather_by_hops(): lax.ppermute(held, axis, [(i, (i + 1) % peers) for i in range(peers)])  47.3 us
    dot_general x4, matrix products, contract_last(): lax.dot_general(left, right, (((1,), (1,)), ((), ())), preferred_element_...  10 us
    dot_general x4, matrix products, contract_first(): lax.dot_general(left, right, (((0,), (0,)), ((), ())), preferred_element_...  9.16 us
    ppermute x3, starting transfers between devices, gather_by_hops(): lax.ppermute(held, axis, [(i, (i + 1) % peers) for i in range(peers)])  7.99 us
    unnamed x64, local copies, waits for them, and re-layouts  7.59 us
  transfers between devices with their start and end apart: 7, of which 6 were waited for; matrix products, arithmetic and copies ran while one was open for 9% of the time, Pallas kernels for 0%

profile of v1, /device:TPU:0, one launch (start us, length us, event | category | flops | bytes accessed | tf_op | source)
XLA Modules:
  0.0 282.5 jit_solution(2458096142738740568)
XLA Ops:
  7.2 0.0 copy-start
  7.2 0.0 all-gather.2.cloned.1.call-start
  7.2 1.4 copy.42
  8.6 1.2 copy.40
  9.9 0.2 copy.41
  10.1 0.8 multiply_reduce_fusion
  10.8 0.7 fusion
  11.6 0.9 divide_convert_fusion
  12.4 0.1 bitcast_convert_fusion.2
  12.6 0.3 copy.44
  12.9 0.2 copy-done.24
  13.1 0.0 copy-start.20
  13.2 0.0 copy-start.21
  13.2 1.3 convert_reduce_fusion
  14.5 0.3 fusion.55
  14.8 1.1 fusion.49
  15.9 0.0 all-gather.2.cloned.1.call-update
  15.9 0.0 all-reduce.5.cloned.1.call-start
  15.9 3.0 %collective-permute-start = (bf16[1,256,1024]{2,1,0:T(8,128)(2,1)S(1)}, bf16[1,256,1024]{2,1,0:T(8,128)(2,1)S(1)}, u32[]{:S(2)}, u32[]{:S(2)}) collective-permute-start(bf16[1,256,1024]{2,1,0:T(8,128)(2,1)S(1)} %copy-done.1), channel_id=1, source_target_pairs={{0,1},{1,2},{2,3},{3,0},{4,5},{5,6},{6,7},{7,4},{8,9},{9,10},{10,1... | collective-permute-start | bytes 1572872 | tf_op jit(solution)/shard_map/ppermute | solution.py:13
  19.0 15.9 %collective-permute-done = bf16[1,256,1024]{2,1,0:T(8,128)(2,1)S(1)} collective-permute-done((bf16[1,256,1024]{2,1,0:T(8,128)(2,1)S(1)}, bf16[1,256,1024]{2,1,0:T(8,128)(2,1)S(1)}, u32[]{:S(2)}, u32[]{:S(2)}) %collective-permute-start) | collective-permute-done | bytes 524320 | tf_op jit(solution)/shard_map/ppermute | solution.py:13
  34.8 2.5 collective-permute-start.1
  37.3 16.8 %collective-permute-done.1 = bf16[1,256,1024]{2,1,0:T(8,128)(2,1)S(1)} collective-permute-done((bf16[1,256,1024]{2,1,0:T(8,128)(2,1)S(1)}, bf16[1,256,1024]{2,1,0:T(8,128)(2,1)S(1)}, u32[]{:S(2)}, u32[]{:S(2)}) %collective-permute-start.1) | collective-permute-done | bytes 524320 | tf_op jit(solution)/shard_map/ppermute | solution.py:13
  54.1 2.5 collective-permute-start.2
  56.6 14.6 %collective-permute-done.2 = bf16[1,256,1024]{2,1,0:T(8,128)(2,1)} collective-permute-done((bf16[1,256,1024]{2,1,0:T(8,128)(2,1)S(1)}, bf16[1,256,1024]{2,1,0:T(8,128)(2,1)}, u32[]{:S(2)}, u32[]{:S(2)}) %collective-permute-start.2) | collective-permute-done | bytes 524320 | tf_op jit(solution)/shard_map/ppermute | solution.py:13
  71.3 1.1 constant_dynamic-update-slice_fusion.7
  72.5 0.0 copy-start.8
  72.5 0.0 copy-start.11
  72.5 1.2 constant_dynamic-update-slice_fusion.3
  73.9 1.9 copy-done.18
  75.8 2.6 fusion.27
  78.5 3.3 %fusion.31 = f32[4,256,512]{2,1,0:T(8,128)S(1)} fusion(bf16[4,256,1024]{2,1,0:T(8,128)(2,1)} %all-gather.2.cloned.1.call-done, bf16[4,1024]{1,0:T(4,128)(2,1)S(1)} %get-tuple-element.19, bf16[1024,512]{1,0:T(8,128)(2,1)S(1)} %copy-done.4, bf16[1024,512]{1,0:T(8,128)(2,1)} %param.22), kind=kOutput, calls=%fused_computation.55 | convolution fusion | flops 1076887552 | bytes 6299648 | tf_op jit(solution)/shard_map/dot_general | solution.py:99
  81.8 1.9 fusion.81
  83.7 4.8 %fusion.8 = bf16[4,256,512]{2,1,0:T(8,128)(2,1)S(1)} fusion(f32[4,256,512]{2,1,0:T(8,128)S(1)} %get-tuple-element.28, u8[256,512]{1,0:T(8,128)(4,1)S(1)} %get-tuple-element.7, u8[256,512]{1,0:T(8,128)(4,1)S(1)} %get-tuple-element.6), kind=kLoop, calls=%fused_computation.18 | loop fusion | flops 36700160 | bytes 3407872 | tf_op jit(solution)/shard_map/convert_element_type | solution.py:105
  88.5 0.0 copy-start.9
  88.5 2.3 bitcast_convert_fusion
  90.8 2.4 fusion.5
  93.2 2.1 fusion.14
  95.3 0.0 copy-start.2
  95.3 0.0 copy-start.5
  95.3 2.3 bitcast_convert_fusion.1
  97.5 2.3 fusion.3
  99.8 0.0 all-reduce.5.cloned.1.call-update
  99.8 0.3 reduce-scatter.9.cloned.1.call-start
  100.1 0.0 copy-start.3
  100.1 0.0 copy-start.6
  100.1 0.0 copy-start.7
  100.1 2.7 fusion.62
  102.8 2.6 add_convert_fusion
  105.5 0.0 reduce-scatter.9.cloned.1.call-update
  105.5 0.0 reduce-scatter.7.cloned.1.call-start
  105.5 0.0 copy-start.10
  105.5 0.0 copy-start.12
  105.6 2.7 fusion.60
  108.3 2.6 add_convert_fusion.1
  110.9 0.0 reduce-scatter.7.cloned.1.call-update
  110.9 86.2 %all-reduce.5.cloned.1.call-done = (bf16[1024,512]{1,0:T(8,128)(2,1)}, bf16[1024,512]{1,0:T(8,128)(2,1)}, bf16[512,1024]{1,0:T(8,128)(2,1)}, bf16[512,1024]{1,0:T(8,128)(2,1)}) async-done(((bf16[1024,512]{1,0:T(8,128)(2,1)}, bf16[1024,512]{1,0:T(8,128)(2,1)}, bf16[512,1024]{1,0:T(8,128)(2,1)}, bf16[512,1024]{1,0:T(8,128)(2,1)}), (bf16[1024,512]{1,0:T(8,128)(2,1)}, bf16[1024,512]{1,0:T(8,128)(2,1)}, ...) | async-done | bytes 4194320 | tf_op jit(solution)/shard_map/psum | solution.py:150
  197.0 2.9 %convert_element_type.173 = f32[1024,512]{1,0:T(8,128)} convert(bf16[1024,512]{1,0:T(8,128)(2,1)} %get-tuple-element.10) | non-fusion elementwise | flops 524288 | bytes 3145728 | tf_op jit(solution)/shard_map/convert_element_type | solution.py:150
  200.0 1.6 convert_element_type.175
  201.6 1.6 convert_element_type.177
  203.2 1.6 convert_element_type.179
  204.7 30.6 %reduce-scatter.9.cloned.1.call-done = bf16[1,256,1024]{2,1,0:T(8,128)(2,1)} async-done(((bf16[4,256,1024]{2,1,0:T(8,128)(2,1)}), bf16[1,256,1024]{2,1,0:T(8,128)(2,1)}) %reduce-scatter.9.cloned.1.call-update) | async-done | bytes 524304
  235.3 1.4 fusion.65
  236.7 36.6 %reduce-scatter.7.cloned.1.call-done = bf16[1,256,1024]{2,1,0:T(8,128)(2,1)} async-done(((bf16[4,256,1024]{2,1,0:T(8,128)(2,1)}), bf16[1,256,1024]{2,1,0:T(8,128)(2,1)}) %reduce-scatter.7.cloned.1.call-update) | async-done | bytes 524304
  273.4 2.6 fusion.54
  (54 shorter events, 0.3 us)
Async XLA Ops:
  7.2 74.6 %copy-start = (bf16[1024,512]{1,0:T(8,128)(2,1)S(1)}, bf16[1024,512]{1,0:T(8,128)(2,1)}, u32[]{:S(2)}) copy-start(bf16[1024,512]{1,0:T(8,128)(2,1)} %param.21) | copy-start | bytes 3145732
  7.2 2.7 copy-start.17
  7.2 71.3 %all-gather.2.cloned.1.call-start = ((), (), s32[]{:S(2)}) async-start(), calls=%async_computation.2 | async-start | bytes 2621440 | tf_op jit(solution)/shard_map/all_gather | solution.py:93
  12.4 0.7 copy-start.24
  13.1 2.8 copy-start.1
  13.1 24.2 %copy-start.22 = (s32[4,512]{1,0:T(4,128)S(1)}, s32[4,512]{1,0:T(4,128)}, u32[]{:S(2)}) copy-start(s32[4,512]{1,0:T(4,128)} %param.28) | copy-start | bytes 24580
  13.1 43.5 %copy-start.23 = (s32[4,512]{1,0:T(4,128)S(1)}, s32[4,512]{1,0:T(4,128)}, u32[]{:S(2)}) copy-start(s32[4,512]{1,0:T(4,128)} %param.29) | copy-start | bytes 24580
  13.1 43.5 %copy-start.20 = (s32[4,1024]{1,0:T(4,128)S(1)}, s32[4,1024]{1,0:T(4,128)}, u32[]{:S(2)}) copy-start(s32[4,1024]{1,0:T(4,128)} %param.27) | copy-start | bytes 49156
  13.2 43.5 %copy-start.21 = (s32[4,1024]{1,0:T(4,128)S(1)}, s32[4,1024]{1,0:T(4,128)}, u32[]{:S(2)}) copy-start(s32[4,1024]{1,0:T(4,128)} %param.30) | copy-start | bytes 49156
  15.9 181.2 %all-reduce.5.cloned.1.call-start = ((), (), s32[]{:S(2)}) async-start(), calls=%async_computation.5 | async-start | bytes 8388608 | tf_op jit(solution)/shard_map/psum | solution.py:150
  15.9 18.9 %collective-permute-start = (bf16[1,256,1024]{2,1,0:T(8,128)(2,1)S(1)}, bf16[1,256,1024]{2,1,0:T(8,128)(2,1)S(1)}, u32[]{:S(2)}, u32[]{:S(2)}) collective-permute-start(bf16[1,256,1024]{2,1,0:T(8,128)(2,1)S(1)} %copy-done.1), channel_id=1, source_target_pairs={{0,1},{1,2},{2,3},{3,0},{4,5},{5,6},{6,7},{7,4},{8,9},{9,10},{10,1... | collective-permute-start | bytes 1572872 | tf_op jit(solution)/shard_map/ppermute | solution.py:13
  34.8 19.3 %collective-permute-start.1 = (bf16[1,256,1024]{2,1,0:T(8,128)(2,1)S(1)}, bf16[1,256,1024]{2,1,0:T(8,128)(2,1)S(1)}, u32[]{:S(2)}, u32[]{:S(2)}) collective-permute-start(bf16[1,256,1024]{2,1,0:T(8,128)(2,1)S(1)} %collective-permute-done), channel_id=1, source_target_pairs={{0,1},{1,2},{2,3},{3,0},{4,5},{5,6},{6,7},{7,4},{8,9},{9,10},{10,1... | collective-permute-start | bytes 1572872 | tf_op jit(solution)/shard_map/ppermute | solution.py:13
  54.1 17.2 %collective-permute-start.2 = (bf16[1,256,1024]{2,1,0:T(8,128)(2,1)S(1)}, bf16[1,256,1024]{2,1,0:T(8,128)(2,1)}, u32[]{:S(2)}, u32[]{:S(2)}) collective-permute-start(bf16[1,256,1024]{2,1,0:T(8,128)(2,1)S(1)} %collective-permute-done.1), channel_id=1, source_target_pairs={{0,1},{1,2},{2,3},{3,0},{4,5},{5,6},{6,7},{7,4},{8,9},{9,10},{10,1... | collective-permute-start | bytes 1572872 | tf_op jit(solution)/shard_map/ppermute | solution.py:13
  72.5 3.3 %copy-start.8 = (bf16[512,1024]{1,0:T(8,128)(2,1)S(1)}, bf16[512,1024]{1,0:T(8,128)(2,1)}, u32[]{:S(2)}) copy-start(bf16[512,1024]{1,0:T(8,128)(2,1)} %param.26) | copy-start | bytes 3145732
  72.5 3.3 %copy-start.11 = (bf16[512,1024]{1,0:T(8,128)(2,1)S(1)}, bf16[512,1024]{1,0:T(8,128)(2,1)}, u32[]{:S(2)}) copy-start(bf16[512,1024]{1,0:T(8,128)(2,1)} %param.25) | copy-start | bytes 3145732
  73.9 1.9 copy-start.18
  75.8 2.6 copy-start.4
  78.5 3.3 %copy-start.25 = (bf16[4,256,1024]{2,1,0:T(8,128)(2,1)S(1)}, bf16[4,256,1024]{2,1,0:T(8,128)(2,1)}, u32[]{:S(2)}) copy-start(bf16[4,256,1024]{2,1,0:T(8,128)(2,1)} %all-gather.2.cloned.1.call-done) | copy-start | bytes 6291460
  81.8 6.7 %copy-start.19 = (bf16[8,256,1024]{2,1,0:T(8,128)(2,1)S(1)}, bf16[8,256,1024]{2,1,0:T(8,128)(2,1)}, u32[]{:S(2)}) copy-start(bf16[8,256,1024]{2,1,0:T(8,128)(2,1)} %copy-done.18) | copy-start | bytes 12582916
  88.5 2.3 copy-start.9
  90.8 2.4 copy-start.16
  90.8 2.4 copy-start.26
  95.3 2.3 copy-start.2
  95.3 2.3 copy-start.5
  99.8 135.5 %reduce-scatter.9.cloned.1.call-start = ((), (), s32[]{:S(2)}) async-start(), calls=%async_computation.4 | async-start | bytes 2621440
  100.1 2.7 copy-start.3
  100.1 2.7 copy-start.6
  100.1 2.7 copy-start.7
  105.5 167.9 %reduce-scatter.7.cloned.1.call-start = ((), (), s32[]{:S(2)}) async-start(), calls=%async_computation.3 | async-start | bytes 2621440
  105.5 2.7 copy-start.10
  105.5 2.7 copy-start.12
  197.0 2.9 %copy-start.15 = (bf16[1024,512]{1,0:T(8,128)(2,1)S(1)}, bf16[1024,512]{1,0:T(8,128)(2,1)}, u32[]{:S(2)}) copy-start(bf16[1024,512]{1,0:T(8,128)(2,1)} %get-tuple-element.11) | copy-start | bytes 3145732
  200.0 1.6 copy-start.14
  201.6 1.6 copy-start.13
Sparse Core Ops, SparseCore 0:
  16.0 50.9 all-gather.1
  99.9 97.0 all-reduce.4
  200.0 35.2 reduce-scatter.8
  238.1 35.1 reduce-scatter.6
